TPU v7x, 128 devices: a whole 4x4x4 slice. The times are simulated.
128 devices in a mesh: shard: 8 (over x, core), replica: 16 (over z, y).
Axes of the slice: x: 4, y: 4, z: 4, core: 2. Of those that a mesh axis runs over, the one named last changes fastest.
Arguments:
- gradients: bfloat16 [16, 128, 512, 512], P('replica', 'shard'), may hold values from -3 to 3
- first_moment: float32 [128, 512, 512], P(('shard', 'replica')), may hold values from -6 to 6
- second_moment: float32 [128, 512, 512], P(('shard', 'replica')), may hold values from 0.25 to 4
- left_stat: float32 [128, 512, 512], P(('shard', 'replica')), as said below
- right_stat: float32 [128, 512, 512], P(('shard', 'replica')), as said below
- left_basis: float32 [128, 512, 512], P(('shard', 'replica')), as said below
- right_basis: float32 [128, 512, 512], P(('shard', 'replica')), as said below
- refresh_flags: int32 [128], replicated, may hold values from 0 to 1, as said below
Outputs:
- direction: bfloat16 [128, 512, 512], P('shard')
- new_first: float32 [128, 512, 512], P(('shard', 'replica'))
- new_second: float32 [128, 512, 512], P(('shard', 'replica'))
- new_left: float32 [128, 512, 512], P(('shard', 'replica'))
- new_right: float32 [128, 512, 512], P(('shard', 'replica'))
- new_left_basis: float32 [128, 512, 512], P(('shard', 'replica'))
- new_right_basis: float32 [128, 512, 512], P(('shard', 'replica'))
Inputs may be any that keep to these rules, and one draw needn't show every extreme that they name: Write b = ((p * 16 + q)) + j. For every q, j and k, exactly one of the two blocks with p = 2 k and p = 2 k + 1 has refresh_flags[b] = 1. `left_stat`: every block is symmetric positive definite with all eigenvalues 1 or more. `right_stat`: every block is symmetric positive definite with all eigenvalues 1 or more. `left_basis`: every block is an orthogonal matrix. `right_basis`: every block is an orthogonal matrix.
All inputs are finite; a program needn't handle non-finite values.
Results may differ from a plain program's by a relative error of at most 0.012.
Values may be sent and summed in bfloat16 or wider, within the bound.
No kernel may reach another device: no remote copies, remote signals or barrier semaphores. Data moves between devices by JAX's collectives and lax.ppermute only.
A program may use at most 128 MiB of HBM per device.

v0:
```python
import jax
import jax.numpy as jnp
from jax import lax
from jax.sharding import PartitionSpec as P

POWER = 2


beta_one = 0.95
beta_two = 0.95
epsilon = 1e-08
bias_step = 10.0


def swapped(block, axis, stride):
    count = lax.axis_size(axis)
    route = []
    for low in range(count):
        high = low | 1 << stride
        if high != low and high < count:
            route += [(low, high), (high, low)]
    return lax.ppermute(block, axis, route)


def highest(left_side, right_side):
    return jnp.dot(
        left_side, right_side, precision=lax.Precision.HIGHEST, preferred_element_type=jnp.float32
    )


def orthonormal(matrix):
    gram = highest(matrix.T, matrix)
    lower_factor = jnp.linalg.cholesky(gram)
    return jax.scipy.linalg.solve_triangular(lower_factor, matrix.T, lower=True).T


def power_step(factor, basis):
    for repeat in range(POWER):
        product = jnp.dot(
            factor.astype(jnp.bfloat16),
            basis.astype(jnp.bfloat16),
            preferred_element_type=jnp.float32,
        )
        basis = orthonormal(product)
    return basis


def local(
    gradients,
    first_moment,
    second_moment,
    left_stat,
    right_stat,
    left_basis,
    right_basis,
    refresh_flags,
):
    replica_count = lax.axis_size("replica")
    shard_pos = lax.axis_index("shard")
    replica_pos = lax.axis_index("replica")
    summed = lax.psum_scatter(gradients, "replica", scatter_dimension=1, tiled=True).astype(
        jnp.float32
    )[0]
    per_device = summed.shape[0]
    block_side = summed.shape[1]
    low_grad = summed.astype(jnp.bfloat16)
    left_new = beta_two * left_stat + (1.0 - beta_two) / block_side * jnp.einsum(
        "kij,klj->kil", low_grad, low_grad, preferred_element_type=jnp.float32
    )
    right_new = beta_two * right_stat + (1.0 - beta_two) / block_side * jnp.einsum(
        "kji,kjl->kil", low_grad, low_grad, preferred_element_type=jnp.float32
    )
    owner_id = shard_pos * replica_count + replica_pos
    own_flags = lax.dynamic_slice_in_dim(refresh_flags, owner_id * per_device, per_device)
    renewed = (own_flags == 1)[:, None, None]
    partner_id = (shard_pos ^ 1) * replica_count + replica_pos
    partner_flags = lax.dynamic_slice_in_dim(refresh_flags, partner_id * per_device, per_device)
    pair_out = jnp.stack([right_new, right_basis], 1).astype(jnp.bfloat16)
    outgoing = jnp.where(renewed[:, :, :, None], pair_out, jnp.zeros_like(pair_out))
    incoming = swapped(outgoing, "shard", 0)
    position = 0
    lefts = [
        lax.cond(
            own_flags[position] == 1,
            lambda: power_step(left_new[position], left_basis[position]),
            lambda: left_basis[position],
        )
    ]
    helped = [
        lax.cond(
            partner_flags[position] == 1,
            lambda: power_step(incoming[position, 0], incoming[position, 1]),
            lambda: jnp.zeros(incoming.shape[2:], jnp.float32),
        )
    ]
    basis_left = jnp.stack(lefts, 0)
    arrived = swapped(jnp.stack(helped, 0).astype(jnp.bfloat16), "shard", 0).astype(jnp.float32)
    basis_right = jnp.where(renewed, arrived, right_basis)
    position = 0
    carried_list = [
        lax.cond(
            own_flags[position] == 1,
            lambda: highest(
                highest(
                    highest(basis_left[position].T, left_basis[position]), first_moment[position]
                ),
                highest(right_basis[position].T, basis_right[position]),
            ),
            lambda: first_moment[position],
        )
    ]
    carried = jnp.stack(carried_list, 0)
    rotated = jnp.einsum("kji,kjl->kil", basis_left, summed, precision=lax.Precision.HIGHEST)
    rotated = jnp.einsum("kil,klm->kim", rotated, basis_right, precision=lax.Precision.HIGHEST)
    moment_new = beta_one * carried + (1.0 - beta_one) * rotated
    second_new = beta_two * second_moment + (1.0 - beta_two) * rotated * rotated
    scaled = (
        moment_new
        / (1.0 - beta_one**bias_step)
        / (jnp.sqrt(second_new / (1.0 - beta_two**bias_step)) + epsilon)
    )
    outward = jnp.einsum("kij,kjl->kil", basis_left, scaled, precision=lax.Precision.HIGHEST)
    outward = jnp.einsum("kil,kml->kim", outward, basis_right, precision=lax.Precision.HIGHEST)
    gathered = lax.all_gather(outward.astype(jnp.bfloat16), "replica", axis=0, tiled=True)
    return (gathered, moment_new, second_new, left_new, right_new, basis_left, basis_right)


def solution(mesh):
    in_specs = (
        P("replica", "shard", None, None),
        P(("shard", "replica"), None, None),
        P(("shard", "replica"), None, None),
        P(("shard", "replica"), None, None),
        P(("shard", "replica"), None, None),
        P(("shard", "replica"), None, None),
        P(("shard", "replica"), None, None),
        P(),
    )
    out_specs = (
        P("shard", None, None),
        P(("shard", "replica"), None, None),
        P(("shard", "replica"), None, None),
        P(("shard", "replica"), None, None),
        P(("shard", "replica"), None, None),
        P(("shard", "replica"), None, None),
        P(("shard", "replica"), None, None),
    )
    return jax.shard_map(local, mesh=mesh, in_specs=in_specs, out_specs=out_specs, check_vma=False)
```

profile of v0, /device:TPU:1, one launch (start us, length us, event | category | flops | bytes accessed | tf_op | source)
XLA Modules:
  0.0 849.1 jit_solution(13793447143394163881)
XLA Ops:
  11.1 88.5 %reduce-scatter.7.cloned.1.call-done = bf16[1,1,512,512]{3,2,1,0:T(8,128)(2,1)} async-done(((bf16[1,16,512,512]{3,2,1,0:T(8,128)(2,1)}), bf16[1,1,512,512]{3,2,1,0:T(8,128)(2,1)}) %reduce-scatter.7.cloned.1.call-update) | async-done | bytes 524304
  105.9 318.5 %conditional.4 = (bf16[512,512]{0,1:T(8,128)(2,1)S(1)}) conditional(s32[]{:T(128)} %bitcast.62, () %tuple.33, bf16[1,2,512,512]{3,2,1,0:T(8,128)(2,1)} %collective-permute-done), branch_computations={%region_11.14_spmd, %region_12.15_spmd} | conditional | flops 6586237440 | bytes 55583216 | solution.py:90
  113.3 11.7 %cholesky.606 = f32[128,128]{1,0:T(8,128)S(1)} custom-call(f32[128,128]{1,0:T(8,128)S(1)} %cholesky.772), custom_call_target="Cholesky" | custom-call | tf_op jit(solution)/shard_map/cond/branch_1_fun/jit(cholesky)/cholesky | solution.py:33
  125.0 9.8 %custom-call.43 = f32[1,128,128]{1,2,0:T(8,128)S(1)} custom-call(f32[1,128,128]{2,1,0:T(8,128)S(1)} %get-tuple-element.187), custom_call_target="InvertDiagBlocksLowerTriangular" | custom-call | tf_op jit(solution)/shard_map/cond/branch_1_fun/jit(cholesky)/cholesky | solution.py:33
  137.5 12.0 %cholesky.625 = f32[128,128]{1,0:T(8,128)S(1)} custom-call(f32[128,128]{1,0:T(8,128)S(1)} %cholesky.776), custom_call_target="Cholesky" | custom-call | tf_op jit(solution)/shard_map/cond/branch_1_fun/jit(cholesky)/cholesky | solution.py:33
  151.4 9.8 %custom-call.44 = f32[1,128,128]{1,2,0:T(8,128)S(1)} custom-call(f32[1,128,128]{2,1,0:T(8,128)S(1)} %get-tuple-element.184), custom_call_target="InvertDiagBlocksLowerTriangular" | custom-call | tf_op jit(solution)/shard_map/cond/branch_1_fun/jit(cholesky)/cholesky | solution.py:33
  162.8 11.7 %cholesky.646 = f32[128,128]{1,0:T(8,128)S(1)} custom-call(f32[128,128]{1,0:T(8,128)S(1)} %cholesky.781), custom_call_target="Cholesky" | custom-call | tf_op jit(solution)/shard_map/cond/branch_1_fun/jit(cholesky)/cholesky | solution.py:33
  175.9 9.8 %custom-call.45 = f32[1,128,128]{1,2,0:T(8,128)S(1)} custom-call(f32[1,128,128]{2,1,0:T(8,128)S(1)} %get-tuple-element.181), custom_call_target="InvertDiagBlocksLowerTriangular" | custom-call | tf_op jit(solution)/shard_map/cond/branch_1_fun/jit(cholesky)/cholesky | solution.py:33
  187.1 23.3 %cholesky.663 = f32[128,128]{1,0:T(8,128)S(1)} custom-call(f32[128,128]{1,0:T(8,128)S(1)} %convolution_subtract_fusion.23), custom_call_target="Cholesky" | custom-call | tf_op jit(solution)/shard_map/cond/branch_1_fun/jit(cholesky)/cholesky | solution.py:33
  212.9 11.6 %while.10 = (s32[]{:T(128)}, f32[512,512]{1,0:T(8,128)}, s32[4,2]{0,1:T(2,128)S(1)}, f32[4,128,128]{2,1,0:T(8,128)S(1)}, s32[]{:T(128)}) while((s32[]{:T(128)}, f32[512,512]{1,0:T(8,128)}, s32[4,2]{0,1:T(2,128)S(1)}, f32[4,128,128]{2,1,0:T(8,128)S(1)}, s32[]{:T(128)}) %tuple.131), condition=%wide.while_cond.clone.1, body=%wide.while_body.clone.1.sunk | while | flops 2 | bytes 131189 | solution.py:34
  224.5 39.3 %custom-call.46 = f32[4,128,128]{1,2,0:T(8,128)S(1)} custom-call(f32[4,128,128]{2,1,0:T(8,128)S(1)} %get-tuple-element.73), custom_call_target="InvertDiagBlocksLowerTriangular" | custom-call | tf_op jit(solution)/shard_map/cond/branch_1_fun/jit(_solve_triangular)/triangular_solve | solution.py:34
  278.4 11.7 %cholesky.678 = f32[128,128]{1,0:T(8,128)S(1)} custom-call(f32[128,128]{1,0:T(8,128)S(1)} %cholesky.785), custom_call_target="Cholesky" | custom-call | tf_op jit(solution)/shard_map/cond/branch_1_fun/jit(cholesky)/cholesky | solution.py:33
  290.7 10.2 %custom-call.47 = f32[1,128,128]{1,2,0:T(8,128)S(1)} custom-call(f32[1,128,128]{2,1,0:T(8,128)S(1)} %get-tuple-element.177), custom_call_target="InvertDiagBlocksLowerTriangular" | custom-call | tf_op jit(solution)/shard_map/cond/branch_1_fun/jit(cholesky)/cholesky | solution.py:33
  303.6 11.7 %cholesky.697 = f32[128,128]{1,0:T(8,128)S(1)} custom-call(f32[128,128]{1,0:T(8,128)S(1)} %cholesky.789), custom_call_target="Cholesky" | custom-call | tf_op jit(solution)/shard_map/cond/branch_1_fun/jit(cholesky)/cholesky | solution.py:33
  317.3 9.8 %custom-call.48 = f32[1,128,128]{1,2,0:T(8,128)S(1)} custom-call(f32[1,128,128]{2,1,0:T(8,128)S(1)} %get-tuple-element.174), custom_call_target="InvertDiagBlocksLowerTriangular" | custom-call | tf_op jit(solution)/shard_map/cond/branch_1_fun/jit(cholesky)/cholesky | solution.py:33
  328.6 11.7 %cholesky.718 = f32[128,128]{1,0:T(8,128)S(1)} custom-call(f32[128,128]{1,0:T(8,128)S(1)} %cholesky.794), custom_call_target="Cholesky" | custom-call | tf_op jit(solution)/shard_map/cond/branch_1_fun/jit(cholesky)/cholesky | solution.py:33
  341.7 9.9 %custom-call.49 = f32[1,128,128]{1,2,0:T(8,128)S(1)} custom-call(f32[1,128,128]{2,1,0:T(8,128)S(1)} %get-tuple-element.171), custom_call_target="InvertDiagBlocksLowerTriangular" | custom-call | tf_op jit(solution)/shard_map/cond/branch_1_fun/jit(cholesky)/cholesky | solution.py:33
  353.0 11.7 %cholesky.735 = f32[128,128]{1,0:T(8,128)S(1)} custom-call(f32[128,128]{1,0:T(8,128)S(1)} %convolution_subtract_fusion.22), custom_call_target="Cholesky" | custom-call | tf_op jit(solution)/shard_map/cond/branch_1_fun/jit(cholesky)/cholesky | solution.py:33
  367.2 11.6 %while.11 = (s32[]{:T(128)}, f32[512,512]{1,0:T(8,128)}, s32[4,2]{0,1:T(2,128)S(1)}, f32[4,128,128]{2,1,0:T(8,128)S(1)}, s32[]{:T(128)}) while((s32[]{:T(128)}, f32[512,512]{1,0:T(8,128)}, s32[4,2]{0,1:T(2,128)S(1)}, f32[4,128,128]{2,1,0:T(8,128)S(1)}, s32[]{:T(128)}) %tuple.159), condition=%wide.while_cond.clone.2, body=%wide.while_body.clone.2.sunk | while | flops 2 | bytes 131189 | solution.py:34
  378.8 39.3 %custom-call.50 = f32[4,128,128]{1,2,0:T(8,128)S(1)} custom-call(f32[4,128,128]{2,1,0:T(8,128)S(1)} %get-tuple-element.74), custom_call_target="InvertDiagBlocksLowerTriangular" | custom-call | tf_op jit(solution)/shard_map/cond/branch_1_fun/jit(_solve_triangular)/triangular_solve | solution.py:34
  428.4 10.6 %conditional.3 = (f32[512,512]{0,1:T(8,128)S(1)}, f32[1,512,512]{1,2,0:T(8,128)}) conditional(s32[]{:T(128)} %convert_element_type.74, (f32[1,512,512]{2,1,0:T(8,128)S(1)}) %tuple.156, (f32[1,512,512]{2,1,0:T(8,128)}, f32[1,512,512]{2,1,0:T(8,128)S(1)}) %tuple.157), branch_computations={%region_1.2_spmd, %region_2.13_spmd} | conditional | flops 6585713152 | bytes 58991096 | solution.py:83
  448.4 4.4 fusion.169
  460.5 373.8 %all-gather.3.cloned.1.call-done = bf16[8192,512]{1,0:T(8,128)(2,1)} async-done(((bf16[512,512]{1,0:T(8,128)(2,1)}), bf16[8192,512]{1,0:T(8,128)(2,1)}) %all-gather.3.cloned.1.call-update) | async-done | bytes 8388624 | tf_op jit(solution)/shard_map/all_gather | solution.py:124
  834.3 7.5 copy.107
  (135 shorter events, 100.1 us)
Async XLA Ops:
  7.2 92.4 %copy-start.11 = (f32[1,512,512]{2,1,0:T(8,128)S(1)}, f32[1,512,512]{2,1,0:T(8,128)}, u32[]{:S(2)}) copy-start(f32[1,512,512]{2,1,0:T(8,128)} %param.21) | copy-start | bytes 3145732
  7.2 3.8 copy-start.3
  7.2 2.5 copy-start.12
  7.2 92.3 %reduce-scatter.7.cloned.1.call-start = ((), (), s32[]{:S(2)}) async-start(), calls=%async_computation.2 | async-start | bytes 8912896
  9.7 824.6 %all-gather.3.cloned.1.call-start = ((), (), s32[]{:S(2)}) async-start(), calls=%async_computation.1 | async-start | bytes 8912896 | tf_op jit(solution)/shard_map/all_gather | solution.py:124
  101.2 4.7 copy-start.5
  101.4 4.5 collective-permute-start
  105.9 322.5 %copy-start.1 = (f32[1,512,512]{2,1,0:T(8,128)S(1)}, f32[1,512,512]{2,1,0:T(8,128)}, u32[]{:S(2)}) copy-start(f32[1,512,512]{2,1,0:T(8,128)} %param.22) | copy-start | bytes 3145732
  112.3 1.0 copy-start.6
  277.4 1.0 copy-start.8
  425.4 16.6 %collective-permute-start.1 = (bf16[1,512,512]{2,1,0:T(8,128)(2,1)}, bf16[1,512,512]{2,1,0:T(8,128)(2,1)}, u32[]{:S(2)}, u32[]{:S(2)}) collective-permute-start(bf16[1,512,512]{2,1,0:T(8,128)(2,1)} %bitcast.229), channel_id=1, source_target_pairs={{0,16},{16,0},{32,48},{48,32},{64,80},{80,64},{96,112},{112,96},{1... | collective-permute-start | bytes 1572872 | tf_op jit(solution)/shard_map/ppermute | solution.py:22
  443.5 9.3 %copy-start = (f32[1,512,512]{2,1,0:T(8,128)}, f32[1,512,512]{2,1,0:T(8,128)S(1)}, u32[]{:S(2)}) copy-start(f32[1,512,512]{2,1,0:T(8,128)S(1)} %convert_select_fusion) | copy-start | bytes 3145732
  444.8 13.3 %copy-start.2 = (f32[512,512]{1,0:T(8,128)S(1)}, f32[512,512]{1,0:T(8,128)}, u32[]{:S(2)}) copy-start(f32[512,512]{1,0:T(8,128)} %get-tuple-element.398) | copy-start | bytes 3145732
  448.3 4.5 copy-start.4
  448.3 4.5 copy-start.10
Sparse Core Ops, SparseCore 0:
  11.4 88.0 reduce-scatter.6
  455.6 378.5 all-gather.2
where the time goes:
time: 860 us; the launch traced here: 849 us
  waiting for transfers between devices  464 us (54%)
  other arithmetic  258 us (30%)
  matrix products  49.4 us (6%)
  local copies, waits for them, and re-layouts  43.3 us (5%)
  loops' own time  16.6 us (2%)
  between operations  16 us (2%)
    all_gather x1, waiting for transfers between devices, local(): lax.all_gather(outward.astype(jnp.bfloat16), 'replica', axis=0, tiled=True)  374 us
    another operation x29, other arithmetic, orthonormal(): lower_factor = jnp.linalg.cholesky(gram)  170 us
    unnamed x3, waiting for transfers between devices  88.5 us
    another operation x5, other arithmetic, orthonormal(): jax.scipy.linalg.solve_triangular(lower_factor, matrix.T, lower=True)  80.8 us
    another operation x27, local copies, waits for them, and re-layouts, orthonormal(): jax.scipy.linalg.solve_triangular(lower_factor, matrix.T, lower=True)  23 us
  transfers between devices with their start and end apart: 4, of which 3 were waited for; matrix products, arithmetic and copies ran while one was open for 2% of the time, Pallas kernels for 0%

commit v1 on v0

v1 whole, which is shorter than its diff:
```python
import jax
import jax.numpy as jnp
from jax import lax
from jax.experimental import pallas as pl
from jax.experimental.pallas import tpu as pltpu
from jax.sharding import PartitionSpec as P

POWER = 2
PANEL = 128
GROUP = 8

beta_one = 0.95
beta_two = 0.95
epsilon = 1e-08
bias_step = 10.0

HIGHEST = lax.Precision.HIGHEST
NN = (((1,), (0,)), ((), ()))
NT = (((1,), (1,)), ((), ()))
TN = (((0,), (0,)), ((), ()))


def mm(left_side, right_side, dims, precision=HIGHEST):
    return lax.dot_general(
        left_side, right_side, dims, precision=precision, preferred_element_type=jnp.float32
    )


def low(left_side, right_side, dims):
    return lax.dot_general(
        left_side.astype(jnp.bfloat16),
        right_side.astype(jnp.bfloat16),
        dims,
        preferred_element_type=jnp.float32,
    )


def swapped(block, axis, stride):
    count = lax.axis_size(axis)
    route = []
    for low_id in range(count):
        high = low_id | 1 << stride
        if high != low_id and high < count:
            route += [(low_id, high), (high, low_id)]
    return lax.ppermute(block, axis, route)


def inverse_factor(rows, out_ref):
    shape = (GROUP, PANEL)
    lane = lax.broadcasted_iota(jnp.int32, shape, 1)
    count = PANEL // GROUP
    for group in range(count):
        start = group * GROUP
        pivot = rows[group]
        lines = [jnp.broadcast_to(pivot[q : q + 1, :], shape) for q in range(GROUP)]
        entry = [
            [
                jnp.broadcast_to(lines[q][:, start + p : start + p + 1], shape) if p >= q else None
                for p in range(GROUP)
            ]
            for q in range(GROUP)
        ]
        inside = (lane >= start) & (lane < start + GROUP)
        lines = [
            jnp.where(inside, jnp.where(lane == start + q, 1.0, 0.0), lines[q])
            for q in range(GROUP)
        ]
        inverse = []
        factor = [[None] * GROUP for _ in range(GROUP)]
        for q in range(GROUP):
            inverse.append(1.0 / entry[q][q])
            for p in range(q + 1, GROUP):
                factor[p][q] = entry[q][p] * inverse[q]
                for r in range(p, GROUP):
                    entry[p][r] = entry[p][r] - factor[p][q] * entry[q][r]
                lines[p] = lines[p] - factor[p][q] * lines[q]
            final = jnp.where(lane < start + GROUP, lines[q] * lax.rsqrt(entry[q][q]), 0.0)
            out_ref[start + q : start + q + 1, :] = final[0:1, :]
        if group + 1 == count:
            break
        solved = [None] * GROUP
        for q in reversed(range(GROUP)):
            value = lines[q] * inverse[q]
            for p in range(q + 1, GROUP):
                value = value - factor[p][q] * solved[p]
            solved[q] = value
        for i in range(group + 1, count):
            below = jnp.where(inside, 0.0, rows[i])
            for q in range(GROUP):
                column = jnp.broadcast_to(rows[i][:, start + q : start + q + 1], shape)
                below = below - column * solved[q]
            rows[i] = below


def refresh_kernel(factor_ref, basis_ref, out_ref, low_ref, gram_ref, prod_ref, inv_ref):
    side = out_ref.shape[0]
    low_ref[...] = basis_ref[...]

    def power(step, carry):
        prod_ref[...] = mm(factor_ref[...], low_ref[...], NN, None)
        gram_ref[...] = mm(prod_ref[...], prod_ref[...], TN)
        for start in range(0, side, PANEL):
            stop = start + PANEL
            rows = [
                gram_ref[i : i + GROUP, start:stop] for i in range(start, stop, GROUP)
            ]
            inverse_factor(rows, inv_ref)
            inv = inv_ref[...]
            ortho = mm(prod_ref[:, start:stop], inv, NT)
            out_ref[:, start:stop] = ortho
            if stop < side:
                upper = mm(inv, gram_ref[start:stop, stop:], NN)
                gram_ref[stop:, stop:] = gram_ref[stop:, stop:] - mm(upper, upper, TN)
                prod_ref[:, stop:] = prod_ref[:, stop:] - mm(ortho, upper, NN)
        low_ref[...] = out_ref[...].astype(jnp.bfloat16)
        return carry

    lax.fori_loop(0, POWER, power, 0)


def refresh(factor, basis):
    side = factor.shape[0]
    return pl.pallas_call(
        refresh_kernel,
        out_shape=(
            jax.ShapeDtypeStruct((side, side), jnp.float32),
            jax.ShapeDtypeStruct((side, side), jnp.bfloat16),
        ),
        in_specs=[pl.BlockSpec(memory_space=pltpu.VMEM)] * 2,
        out_specs=(pl.BlockSpec(memory_space=pltpu.VMEM),) * 2,
        scratch_shapes=[
            pltpu.VMEM((side, side), jnp.float32),
            pltpu.VMEM((side, side), jnp.float32),
            pltpu.VMEM((PANEL, PANEL), jnp.float32),
        ],
        name="refresh",
    )(factor, basis)


def update_kernel(
    flag_ref,
    new_left_ref,
    new_right_ref,
    old_left_ref,
    old_right_ref,
    summed_ref,
    spread_ref,
    first_ref,
    second_ref,
    direction_ref,
    first_out_ref,
    second_out_ref,
    left_out_ref,
    right_out_ref,
):
    renewed = flag_ref[0] == 1
    left = jnp.where(renewed, new_left_ref[...], old_left_ref[...])
    left_out_ref[...] = left
    left = left.astype(jnp.bfloat16)
    right = jnp.where(renewed, new_right_ref[...].astype(jnp.float32), old_right_ref[...])
    right_out_ref[...] = right
    right = right.astype(jnp.bfloat16)
    rotated = low(low(left, summed_ref[...], TN), right, NN)
    carried = low(low(left, spread_ref[...], TN), right, NN)
    carried = jnp.where(renewed, carried, first_ref[...])
    moment_new = beta_one * carried + (1.0 - beta_one) * rotated
    second_new = beta_two * second_ref[...] + (1.0 - beta_two) * rotated * rotated
    first_out_ref[...] = moment_new
    second_out_ref[...] = second_new
    scaled = (
        moment_new
        / (1.0 - beta_one**bias_step)
        / (jnp.sqrt(second_new / (1.0 - beta_two**bias_step)) + epsilon)
    )
    direction_ref[...] = low(low(left, scaled, NN), right, NT).astype(jnp.bfloat16)


def update(flag, *arrays):
    side = arrays[0].shape[0]
    block = jax.ShapeDtypeStruct((side, side), jnp.float32)
    vmem = pl.BlockSpec(memory_space=pltpu.VMEM)
    return pl.pallas_call(
        update_kernel,
        out_shape=(jax.ShapeDtypeStruct((side, side), jnp.bfloat16), block, block, block, block),
        in_specs=[pl.BlockSpec(memory_space=pltpu.SMEM)] + [vmem] * len(arrays),
        out_specs=(vmem,) * 5,
        name="update",
    )(flag, *arrays)


def local(
    gradients,
    first_moment,
    second_moment,
    left_stat,
    right_stat,
    left_basis,
    right_basis,
    refresh_flags,
):
    replica_count = lax.axis_size("replica")
    owner_id = lax.axis_index("shard") * replica_count + lax.axis_index("replica")
    flag = lax.dynamic_slice_in_dim(refresh_flags, owner_id, 1)
    renewed = flag[0] == 1
    old_left, old_right, first = left_basis[0], right_basis[0], first_moment[0]
    arrived_basis = swapped(old_right.astype(jnp.bfloat16), "shard", 0)
    start_basis = jnp.where(renewed, old_left.astype(jnp.bfloat16), arrived_basis)
    spread = mm(mm(old_left, first, NN), old_right, NT).astype(jnp.bfloat16)

    summed = lax.psum_scatter(gradients, "replica", scatter_dimension=1, tiled=True)[0, 0]
    summed, spread, start_basis = lax.optimization_barrier((summed, spread, start_basis))
    side = summed.shape[0]
    weight = (1.0 - beta_two) / side
    right_new = beta_two * right_stat[0] + weight * mm(summed, summed, TN, None)
    left_new = beta_two * left_stat[0] + weight * mm(summed, summed, NT, None)
    arrived_factor = swapped(right_new.astype(jnp.bfloat16), "shard", 0)
    factor = jnp.where(renewed, left_new.astype(jnp.bfloat16), arrived_factor)
    fresh, fresh_low = refresh(factor, start_basis)
    helped = swapped(fresh_low, "shard", 0)
    direction, first_new, second_new, basis_left, basis_right = update(
        flag, fresh, helped, old_left, old_right, summed, spread, first, second_moment[0]
    )
    gathered = lax.all_gather(direction[None], "replica", axis=0, tiled=True)
    return (
        gathered,
        first_new[None],
        second_new[None],
        left_new[None],
        right_new[None],
        basis_left[None],
        basis_right[None],
    )


def solution(mesh):
    owned = P(("shard", "replica"), None, None)
    in_specs = (P("replica", "shard", None, None),) + (owned,) * 6 + (P(),)
    out_specs = (P("shard", None, None),) + (owned,) * 6
    return jax.shard_map(local, mesh=mesh, in_specs=in_specs, out_specs=out_specs, check_vma=False)
```

time: 860 us -> 266 us (0.31); the launches traced: 849 us -> 266 us
  waiting for transfers between devices: 464 us -> 156 us
  other arithmetic: 258 us -> 1.73 us
  Pallas kernels: 0 us -> 69.2 us
  matrix products: 49.4 us -> 10.4 us
  local copies, waits for them, and re-layouts: 43.3 us -> 9.43 us
  loops' own time: 16.6 us -> 0 us
    all_gather x1, waiting for transfers between devices: 374 us -> 70 us  [local(): gathered = lax.all_gather(direction[None], 'replica', axis=0, tiled=True)]
    another operation x36 -> x0, other arithmetic: 251 us -> none  [the longest x29 170 us: orthonormal(): lower_factor = jnp.linalg.cholesky(gram)]
    pallas_call x0 -> x2, Pallas kernels: none -> 69.2 us  [the longest x1 62.3 us: refresh(): pl.pallas_call(refresh_kernel, out_shape=(jax.ShapeDtypeStruct((side, sid...]
    another operation x26 -> x0, matrix products: 24.1 us -> none  [the longest x14 13.2 us: orthonormal(): jax.scipy.linalg.solve_triangular(lower_factor, matrix.T, lower=True)]
    another operation x35 -> x0, local copies, waits for them, and re-layouts: 23.3 us -> none  [the longest x27 23 us: orthonormal(): jax.scipy.linalg.solve_triangular(lower_factor, matrix.T, lower=True)]
    another operation x5 -> x0, loops' own time: 16.6 us -> none  [the longest x1 9.25 us: local(): lax.cond(own_flags[position] == 1, lambda: power_step(left_new[position],...]
    dot_general x10 -> x4, matrix products: 25.3 us -> 10.4 us  [mm(): lax.dot_general(left_side, right_side, dims, precision=precision, preferr...]
  transfers between devices with their start and end apart: 4 -> 5, of which waited for: 3 -> 4; matrix products, arithmetic and copies ran while one was open for 2% -> 3% of each run, Pallas kernels for 0% -> 0%
where the time goes in v1:
time: 266 us
  waiting for transfers between devices  156 us (59%)
  Pallas kernels  69.2 us (26%)
  between operations  14.8 us (6%)
  matrix products  10.4 us (4%)
  local copies, waits for them, and re-layouts  9.43 us (4%)
  starting transfers between devices  3.82 us (1%)
    unnamed x3, waiting for transfers between devices  82.8 us
    all_gather x1, waiting for transfers between devices, local(): gathered = lax.all_gather(direction[None], 'replica', axis=0, tiled=True)  70 us
    pallas_call x1, Pallas kernels, refresh(): pl.pallas_call(refresh_kernel, out_shape=(jax.ShapeDtypeStruct((side, sid...  62.3 us
    dot_general x4, matrix products, mm(): lax.dot_general(left_side, right_side, dims, precision=precision, preferr...  10.4 us
    unnamed x13, local copies, waits for them, and re-layouts  8.77 us
    pallas_call x1, Pallas kernels, update(): pl.pallas_call(update_kernel, out_shape=(jax.ShapeDtypeStruct((side, side...  6.94 us
  transfers between devices with their start and end apart: 5, of which 4 were waited for; matrix products, arithmetic and copies ran while one was open for 3% of the time, Pallas kernels for 0%

profile of v1, /device:TPU:1, one launch (start us, length us, event | category | flops | bytes accessed | tf_op | source)
XLA Modules:
  0.0 265.5 jit_solution(14067787723460593785)
XLA Ops:
  7.2 0.0 copy-start.1
  7.2 0.0 reduce-scatter.7.cloned.1.call-start
  7.3 0.7 reduce-scatter.7.cloned.1.call-update
  7.9 0.0 all-gather.3.cloned.1.call-start
  8.0 0.4 copy-done.1
  8.4 0.9 bitcast_convert_fusion
  9.3 1.4 collective-permute-start
  10.6 0.7 dynamic_slice.3.flag_ref
  12.0 1.8 fusion.3
  13.9 2.7 %convolution_convert_fusion.spread_ref = bf16[512,512]{1,0:T(8,128)(2,1)} fusion(f32[512,512]{1,0:T(8,128)S(1)} %fusion.3, f32[1,512,512]{2,1,0:T(8,128)S(1)} %copy-done.1), kind=kOutput, calls=%fused_computation.4 | convolution fusion | flops 1610874880 | bytes 2621440 | tf_op jit(solution)/shard_map/dot_general | solution.py:24
  16.5 0.9 convert_select_fusion.1.basis_ref
  17.4 82.1 %reduce-scatter.7.cloned.1.call-done = bf16[1,1,512,512]{3,2,1,0:T(8,128)(2,1)} async-done(((bf16[1,16,512,512]{3,2,1,0:T(8,128)(2,1)}), bf16[1,1,512,512]{3,2,1,0:T(8,128)(2,1)}) %reduce-scatter.7.cloned.1.call-update) | async-done | bytes 524304
  99.6 3.0 %fusion.6 = (bf16[512,512]{1,0:T(8,128)(2,1)S(1)}, f32[512,512]{1,0:T(8,128)}) fusion(bf16[512,512]{1,0:T(8,128)(2,1)} %bitcast.37, f32[1,512,512]{2,1,0:T(8,128)} %param.12), kind=kOutput, calls=%fused_computation.12 | convolution fusion | flops 269484032 | bytes 3145728 | tf_op jit(solution)/shard_map/dot_general | solution.py:24
  102.6 2.0 collective-permute-start.1
  104.6 1.5 collective-permute-done.1
  106.1 2.9 %convert_select_fusion = (bf16[512,512]{1,0:T(8,128)(2,1)}, f32[512,512]{1,0:T(8,128)}) fusion(bf16[512,512]{1,0:T(8,128)(2,1)S(1)} %collective-permute-done.1, pred[]{:T(512)} %bitcast, bf16[512,512]{1,0:T(8,128)(2,1)} %bitcast.38, f32[1,512,512]{2,1,0:T(8,128)S(1)} %copy-done.3), kind=kOutput, calls=%fused_computation.5 | convolution fusion | flops 269746176 | bytes 3670017 | tf_op jit(solution)/shard_map/dot_general | solution.py:24
  109.0 62.3 %refresh.1 = (f32[512,512]{1,0:T(8,128)}, bf16[512,512]{1,0:T(8,128)(2,1)}) custom-call(bf16[512,512]{1,0:T(8,128)(2,1)} %get-tuple-element.29.factor_ref, bf16[512,512]{1,0:T(8,128)(2,1)} %convert_select_fusion.1.basis_ref), custom_call_target="tpu_custom_call" | custom-call | tf_op jit(solution)/shard_map/refresh/pallas_call | solution.py:123
  171.3 0.4 collective-permute-start.2
  171.7 1.8 collective-permute-done.2.new_right_ref
  173.4 0.8 copy-done.4
  174.2 6.9 %update.1 = (bf16[512,512]{1,0:T(8,128)(2,1)}, f32[512,512]{1,0:T(8,128)}, f32[512,512]{1,0:T(8,128)}, f32[512,512]{1,0:T(8,128)}, f32[512,512]{1,0:T(8,128)}) custom-call(s32[1]{0:T(128)} %dynamic_slice.3.flag_ref, f32[512,512]{1,0:T(8,128)} %get-tuple-element.19.new_left_ref, bf16[512,512]{1,0:T(8,128)(2,1)} %copy-done.4, f32[512,512]{1,0:T(8,128)} %bitcast.40, ...), custom_call_target="tpu_custom_call" | custom-call | tf_op jit(solution)/shard_map/update/pallas_call | solution.py:182
  181.2 0.0 all-gather.3.cloned.1.call-update
  181.2 70.0 %all-gather.3.cloned.1.call-done = bf16[8192,512]{1,0:T(8,128)(2,1)} async-done(((bf16[512,512]{1,0:T(8,128)(2,1)}), bf16[8192,512]{1,0:T(8,128)(2,1)}) %all-gather.3.cloned.1.call-update) | async-done | bytes 8388624 | tf_op jit(solution)/shard_map/all_gather | solution.py:223
  251.2 7.5 %copy.18 = bf16[16,512,512]{2,1,0:T(8,128)(2,1)} copy(bf16[16,512,512]{2,1,0:T(8,128)(2,1)} %bitcast.42) | data formatting | bytes 16777216
  (10 shorter events, 0.0 us)
Async XLA Ops:
  7.2 1.2 copy-start.1
  7.2 3.5 %copy-start.5 = (s32[128]{0:T(128)S(1)}, s32[128]{0:T(128)}, u32[]{:S(2)}) copy-start(s32[128]{0:T(128)} %param.15) | copy-start | bytes 1540
  7.2 4.8 %copy-start = (f32[1,512,512]{2,1,0:T(8,128)S(1)}, f32[1,512,512]{2,1,0:T(8,128)}, u32[]{:S(2)}) copy-start(f32[1,512,512]{2,1,0:T(8,128)} %param.13) | copy-start | bytes 3145732
  7.2 4.8 %copy-start.2 = (f32[1,512,512]{2,1,0:T(8,128)S(1)}, f32[1,512,512]{2,1,0:T(8,128)}, u32[]{:S(2)}) copy-start(f32[1,512,512]{2,1,0:T(8,128)} %param.9) | copy-start | bytes 3145732
  7.2 92.3 %reduce-scatter.7.cloned.1.call-start = ((), (), s32[]{:S(2)}) async-start(), calls=%async_computation.2 | async-start | bytes 8912896
  7.9 243.2 %all-gather.3.cloned.1.call-start = ((), (), s32[]{:S(2)}) async-start(), calls=%async_computation.1 | async-start | bytes 8912896 | tf_op jit(solution)/shard_map/all_gather | solution.py:223
  9.3 7.3 %collective-permute-start = (bf16[512,512]{1,0:T(8,128)(2,1)}, bf16[512,512]{1,0:T(8,128)(2,1)}, u32[]{:S(2)}, u32[]{:S(2)}) collective-permute-start(bf16[512,512]{1,0:T(8,128)(2,1)} %bitcast_convert_fusion), channel_id=1, source_target_pairs={{0,16},{16,0},{32,48},{48,32},{64,80},{80,64},{96,112},{112,96},{1... | collective-permute-start | bytes 1572872 | tf_op jit(solution)/shard_map/ppermute | solution.py:45
  13.9 92.2 %copy-start.3 = (f32[1,512,512]{2,1,0:T(8,128)S(1)}, f32[1,512,512]{2,1,0:T(8,128)}, u32[]{:S(2)}) copy-start(f32[1,512,512]{2,1,0:T(8,128)} %param.11) | copy-start | bytes 3145732
  102.6 3.5 %collective-permute-start.1 = (bf16[512,512]{1,0:T(8,128)(2,1)S(1)}, bf16[512,512]{1,0:T(8,128)(2,1)S(1)}, u32[]{:S(2)}, u32[]{:S(2)}) collective-permute-start(bf16[512,512]{1,0:T(8,128)(2,1)S(1)} %get-tuple-element.27), channel_id=1, source_target_pairs={{0,16},{16,0},{32,48},{48,32},{64,80},{80,64},{96,112},{112,96},{1... | collective-permute-start | bytes 1572872 | tf_op jit(solution)/shard_map/ppermute | solution.py:45
  171.3 2.1 collective-permute-start.2
  173.4 0.8 copy-start.4
Sparse Core Ops, SparseCore 0:
  11.4 88.0 reduce-scatter.6
  181.3 69.7 all-gather.2
